TPU v7x, 128 devices: a whole 4x4x4 slice. The times are simulated.
128 devices in a mesh: band: 8 (over y, x_lo), chan: 16 (over x_hi, z, core).
Axes of the slice: x: 4 (x_hi: 2, x_lo: 2; x = x_hi * 2 + x_lo), y: 4, z: 4, core: 2. Of those that a mesh axis runs over, the one named last changes fastest.
Arguments:
- coeffs: bfloat16 [2, 8, 1024, 8192], P(None, None, 'chan', 'band'), may hold values from -1100 to 1100, as said below
Outputs:
- coherence: float32 [1024, 1024], P('chan', 'band')
Inputs may be any that keep to these rules, and one draw needn't show every extreme that they name: `coeffs`: finite real and imaginary parts.
All inputs are finite; a program needn't handle non-finite values.
Results may differ from a plain program's by a relative error of at most 0.0003.
Values may be sent and summed in bfloat16 or wider, within the bound.
A program may use at most 192 MiB of HBM per device.

v0:
```python
import jax
import jax.numpy as jnp
from jax import lax
from jax.sharding import PartitionSpec as P

K = 8
W = 16
epsilon = 1e-06


def in_blocks(shard, dim, length):
    dims = shard.shape
    tiles = shard.reshape(*dims[:dim], length, dims[dim] // length, *dims[dim + 1 :])
    return jnp.moveaxis(tiles, dim, 0)


def sent_and_summed(shard, axis, dim):
    length = lax.axis_size(axis)
    tiles = lax.all_to_all(in_blocks(shard, dim, length), axis, 0, 0, tiled=True)
    return jnp.sum(tiles, axis=0)


def body(coeffs):
    num_bands = coeffs.shape[3] // W
    own_width = coeffs.shape[2]
    cycle_size = lax.axis_size("chan")
    own_index = lax.axis_index("chan")
    full_width = own_width * cycle_size
    group_count = lax.axis_size("band")
    scale = jnp.float32(W * K / (num_bands * group_count))
    local_rows = coeffs.reshape(2, K, own_width, num_bands, W)
    paired = jnp.stack((local_rows[1], -local_rows[0]), axis=0)
    left_side = jnp.concatenate((local_rows, paired), axis=2)
    wide_rows = local_rows.astype(jnp.float32)
    own_power = jnp.sum(wide_rows * wide_rows, axis=(0, 1, 4)).T + epsilon
    piece = lax.all_gather(coeffs, "chan", axis=2, tiled=True)
    count = piece.shape[2]
    right_side = piece.reshape(2, K, count, num_bands, W)
    product = jnp.einsum(
        "pkinw,pkjnw->nij", left_side, right_side, preferred_element_type=jnp.float32
    )
    real_part = product[:, :own_width, :]
    imag_part = product[:, own_width:, :]
    wide_piece = right_side.astype(jnp.float32)
    piece_power = jnp.sum(wide_piece * wide_piece, axis=(0, 1, 4)).T + epsilon
    coh_band = (real_part * real_part + imag_part * imag_part) / (
        own_power[:, :, None] * piece_power[:, None, :]
    )
    partial_value = jnp.sum(coh_band, axis=0)
    row_global = lax.broadcasted_iota(jnp.int32, (own_width, full_width), 0) + own_index * own_width
    col_global = lax.broadcasted_iota(jnp.int32, (own_width, full_width), 1)
    partial_value = jnp.where(row_global == col_global, jnp.float32(0.0), partial_value)
    result = sent_and_summed(partial_value, "band", 1)
    return result * scale


def solution(mesh):
    return jax.shard_map(
        body,
        mesh=mesh,
        in_specs=(P(None, None, "chan", "band"),),
        out_specs=P("chan", "band"),
        check_vma=False,
    )
```

profile of v0, /device:TPU:0, one launch (start us, length us, event | category | flops | bytes accessed | tf_op | source)
XLA Modules:
  0.0 327.6 jit_solution(6133088543758207707)
XLA Ops:
  6.5 0.0 copy-start
  6.5 0.0 all-gather.2.cloned.1.call-start
  6.5 4.2 %copy.37 = bf16[2,8,64,1024]{3,1,0,2:T(8,128)(2,1)} copy(bf16[2,8,64,1024]{3,2,1,0:T(8,128)(2,1)} %param.1) | data formatting | bytes 4194304 | tf_op args[0]
  10.7 0.0 all-gather.2.cloned.1.call-update
  10.8 0.0 copy-done
  10.8 3.2 copy.31
  14.0 0.4 multiply_reduce_fusion.1
  14.4 0.2 copy.40
  14.6 0.1 bitcast_reduce_fusion.1
  14.7 4.0 %fusion.14 = (bf16[1,8,64,1024]{2,3,1,0:T(8,128)(2,1)S(1)}, bf16[1,8,64,1024]{2,3,1,0:T(8,128)(2,1)}) fusion(bf16[2,8,64,1024]{2,3,1,0:T(8,128)(2,1)} %copy.31), kind=kLoop, calls=%fused_computation.25 | loop fusion | flops 524288 | bytes 4194304 | tf_op jit(solution)/shard_map/slice | solution.py:32
  18.7 180.3 %all-gather.2.cloned.1.call-done = bf16[2,8,1024,1024]{3,1,0,2:T(8,128)(2,1)} async-done(((bf16[2,8,64,1024]{3,1,0,2:T(8,128)(2,1)}), bf16[2,8,1024,1024]{3,1,0,2:T(8,128)(2,1)}) %all-gather.2.cloned.1.call-update) | async-done | bytes 33554448 | tf_op jit(solution)/shard_map/all_gather | solution.py:36
  199.1 18.3 %multiply_reduce_fusion = f32[1024,1024]{1,0:T(8,128)} fusion(bf16[2,8,1024,1024]{3,1,0,2:T(8,128)(2,1)} %all-gather.2.cloned.1.call-done), kind=kLoop, calls=%fused_computation | loop fusion | flops 49283072 | bytes 37748736 | tf_op jit(solution)/shard_map/reduce_sum | solution.py:45
  217.3 5.3 %copy.41 = f32[1024,1024]{0,1:T(8,128)} copy(f32[1024,1024]{1,0:T(8,128)} %multiply_reduce_fusion) | data formatting | bytes 8388608 | tf_op jit(solution)/shard_map/reduce_sum | solution.py:45
  222.7 3.1 bitcast_reduce_fusion
  225.8 45.1 %copy.38 = bf16[2,8,1024,1024]{2,3,1,0:T(8,128)(2,1)} copy(bf16[2,8,1024,1024]{3,1,0,2:T(8,128)(2,1)} %all-gather.2.cloned.1.call-done) | data formatting | bytes 67108864 | tf_op jit(solution)/shard_map/all_gather | solution.py:36
  271.0 25.2 %fusion.5 = f32[64,128,1024]{2,1,0:T(8,128)} fusion(bf16[2,8,1024,64,16]{2,4,3,1,0:T(8,128)(2,1)} %bitcast.24, bf16[1,8,64,64,16]{2,4,0,3,1:T(8,128)(2,1)} %bitcast.27, bf16[1,8,64,64,16]{2,4,0,3,1:T(8,128)(2,1)S(1)} %bitcast.26, bf16[2,8,64,64,16]{2,4,3,1,0:T(8,128)(2,1)} %bitcast.25), kind=kOutput, calls=%fused_computation.8 | convolution fusion | flops 4307550208 | bytes 71303168 | tf_op jit(solution)/shard_map/pkinw,pkjnw->nij/dot_general | solution.py:39
  296.2 11.9 %fusion.4 = f32[64,1024]{1,0:T(8,128)S(1)} fusion(f32[64,128,1024]{2,1,0:T(8,128)} %fusion.5, f32[64,1024]{1,0:T(8,128)S(1)} %add_bitcast_fusion, f32[64,64]{1,0:T(8,128)S(1)} %add_bitcast_fusion.1), kind=kLoop, calls=%fused_computation.7 | loop fusion | flops 25100288 | bytes 34095104 | tf_op jit(solution)/shard_map/reduce_sum | solution.py:49
  308.1 0.1 bitcast_select_fusion
  308.3 0.1 copy.42
  308.3 11.8 %all_to_all.5 = f32[8,64,128]{2,1,0:T(8,128)S(1)} all-to-all(f32[8,64,128]{2,1,0:T(8,128)S(1)} %copy.42), channel_id=1, replica_groups=mesh['band'=8,'chan'=16] {'band'}, dimensions={0} | all-to-all | bytes 524288 | tf_op jit(solution)/shard_map/all_to_all | solution.py:19
  320.1 0.6 broadcast_multiply_fusion
  (6 shorter events, 0.1 us)
Async XLA Ops:
  6.5 4.2 %copy-start = (bf16[2,8,64,1024]{3,2,1,0:T(8,128)(2,1)S(1)}, bf16[2,8,64,1024]{3,2,1,0:T(8,128)(2,1)}, u32[]{:S(2)}) copy-start(bf16[2,8,64,1024]{3,2,1,0:T(8,128)(2,1)} %param.1) | copy-start | bytes 6291460
  6.5 192.5 %all-gather.2.cloned.1.call-start = ((), (), s32[]{:S(2)}) async-start(), calls=%async_computation.1 | async-start | bytes 35651584 | tf_op jit(solution)/shard_map/all_gather | solution.py:36
Sparse Core Ops, SparseCore 0:
  10.9 188.1 all-gather.1
where the time goes:
time: 329 us; the launch traced here: 328 us
  waiting for transfers between devices  180 us (55%)
  local copies, waits for them, and re-layouts  58.2 us (18%)
  other arithmetic  38.6 us (12%)
  matrix products  25.2 us (8%)
  between operations  13.5 us (4%)
  blocking collectives  11.8 us (4%)
    all_gather x1, waiting for transfers between devices, body(): piece = lax.all_gather(coeffs, 'chan', axis=2, tiled=True)  180 us
    all_gather x1, local copies, waits for them, and re-layouts, body(): piece = lax.all_gather(coeffs, 'chan', axis=2, tiled=True)  45.1 us
    dot_general x1, matrix products, body(): jnp.einsum('pkinw,pkjnw->nij', left_side, right_side, preferred_element_t...  25.2 us
    reduce_sum x2, other arithmetic, body(): piece_power = jnp.sum(wide_piece * wide_piece, axis=(0, 1, 4)).T + epsilon  21.4 us
    reduce_sum x1, other arithmetic, body(): partial_value = jnp.sum(coh_band, axis=0)  11.9 us
    all_to_all x1, blocking collectives, sent_and_summed(): lax.all_to_all(in_blocks(shard, dim, length), axis, 0, 0, tiled=True)  11.8 us
    unnamed x5, local copies, waits for them, and re-layouts  7.43 us
  transfers between devices with their start and end apart: 1, of which 1 were waited for; matrix products, arithmetic and copies ran while one was open for 2% of the time, Pallas kernels for 0%

commit v1 on v0

--- a/solution.py
+++ b/solution.py
@@ -33,7 +33,9 @@
     left_side = jnp.concatenate((local_rows, paired), axis=2)
     wide_rows = local_rows.astype(jnp.float32)
     own_power = jnp.sum(wide_rows * wide_rows, axis=(0, 1, 4)).T + epsilon
-    piece = lax.all_gather(coeffs, "chan", axis=2, tiled=True)
+    piece = jnp.concatenate(
+        lax.all_to_all(jnp.stack([coeffs] * lax.axis_size("chan")), "chan", 0, 0), axis=2
+    )
     count = piece.shape[2]
     right_side = piece.reshape(2, K, count, num_bands, W)
     product = jnp.einsum(

time: 329 us -> 802 us (2.44); the launches traced: 328 us -> 792 us
  waiting for transfers between devices: 180 us -> 517 us
  local copies, waits for them, and re-layouts: 58.2 us -> 196 us
  between operations: 13.5 us -> 0.12 us
  starting transfers between devices: 0.01 us -> 8.19 us
    all_to_all x0 -> x1, waiting for transfers between devices: none -> 517 us  [body(): lax.all_to_all(jnp.stack([coeffs] * lax.axis_size('chan')), 'chan', 0, 0)]
    all_gather x1 -> x0, waiting for transfers between devices: 180 us -> none  [body(): piece = lax.all_gather(coeffs, 'chan', axis=2, tiled=True)]
    another operation x0 -> x2, local copies, waits for them, and re-layouts: none -> 99.1 us  [the longest x1 86.9 us: body(): right_side = piece.reshape(2, K, count, num_bands, W)]
    reshape x0 -> x1, local copies, waits for them, and re-layouts: none -> 77.6 us  [body(): jnp.concatenate(lax.all_to_all(jnp.stack([coeffs] * lax.axis_size('chan')...]
    all_gather x1 -> x0, local copies, waits for them, and re-layouts: 45.1 us -> none  [body(): piece = lax.all_gather(coeffs, 'chan', axis=2, tiled=True)]
    reduce_sum x1 -> x2, local copies, waits for them, and re-layouts: 5.34 us -> 15.7 us  [body(): piece_power = jnp.sum(wide_piece * wide_piece, axis=(0, 1, 4)).T + epsilon]
    all_to_all x0 -> x1, starting transfers between devices: none -> 8.19 us  [body(): lax.all_to_all(jnp.stack([coeffs] * lax.axis_size('chan')), 'chan', 0, 0)]
  transfers between devices with their start and end apart: 1 -> 1, of which waited for: 1 -> 1; matrix products, arithmetic and copies ran while one was open for 2% -> 1% of each run, Pallas kernels for 0% -> 0%
where the time goes in v1:
time: 802 us; the launch traced here: 792 us
  waiting for transfers between devices  517 us (64%)
  local copies, waits for them, and re-layouts  196 us (24%)
  other arithmetic  33.8 us (4%)
  matrix products  25.2 us (3%)
  blocking collectives  11.6 us (1%)
  starting transfers between devices  8.19 us (1%)
    all_to_all x1, waiting for transfers between devices, body(): lax.all_to_all(jnp.stack([coeffs] * lax.axis_size('chan')), 'chan', 0, 0)  517 us
    another operation x1, local copies, waits for them, and re-layouts, body(): right_side = piece.reshape(2, K, count, num_bands, W)  86.9 us
    reshape x1, local copies, waits for them, and re-layouts, body(): jnp.concatenate(lax.all_to_all(jnp.stack([coeffs] * lax.axis_size('chan')...  77.6 us
    dot_general x1, matrix products, body(): jnp.einsum('pkinw,pkjnw->nij', left_side, right_side, preferred_element_t...  25.2 us
    reduce_sum x2, other arithmetic, body(): piece_power = jnp.sum(wide_piece * wide_piece, axis=(0, 1, 4)).T + epsilon  16.6 us
  transfers between devices with their start and end apart: 1, of which 1 were waited for; matrix products, arithmetic and copies ran while one was open for 1% of the time, Pallas kernels for 0%

profile of v1, /device:TPU:0, one launch (start us, length us, event | category | flops | bytes accessed | tf_op | source)
XLA Modules:
  0.0 792.1 jit_solution(12360225404881714423)
XLA Ops:
  0.0 12.2 %stack.5 = bf16[16,2,8,64,1024]{4,3,2,1,0:T(8,128)(2,1)} broadcast(bf16[2,8,64,1024]{3,2,1,0:T(8,128)(2,1)} %param.1), dimensions={1,2,3,4} | broadcast | bytes 35651584 | tf_op jit(solution)/shard_map/stack | solution.py:37
  12.2 0.0 copy-start
  12.2 8.2 %all-to-all-start = ((bf16[16,2,8,64,1024]{4,3,2,1,0:T(8,128)(2,1)}), bf16[16,2,8,64,1024]{4,3,2,1,0:T(8,128)(2,1)}, u32[]{:S(2)}, u32[]{:S(2)}) async-start(bf16[16,2,8,64,1024]{4,3,2,1,0:T(8,128)(2,1)} %stack.5), calls=%async_computation | async-start | bytes 67108864 | tf_op jit(solution)/shard_map/all_to_all | solution.py:37
  20.4 0.0 copy-done
  20.4 3.1 copy.29
  23.5 0.4 multiply_reduce_fusion.1
  23.9 0.2 copy.37
  24.2 0.1 bitcast_reduce_fusion
  24.3 3.9 fusion.14
  28.2 517.5 %all-to-all-done = bf16[16,2,8,64,1024]{4,3,2,1,0:T(8,128)(2,1)} async-done(((bf16[16,2,8,64,1024]{4,3,2,1,0:T(8,128)(2,1)}), bf16[16,2,8,64,1024]{4,3,2,1,0:T(8,128)(2,1)}, u32[]{:S(2)}, u32[]{:S(2)}) %all-to-all-start) | async-done | bytes 33554464 | tf_op jit(solution)/shard_map/all_to_all | solution.py:37
  545.7 13.5 %multiply_reduce_fusion = f32[16,64,1024]{2,1,0:T(8,128)} fusion(bf16[16,2,8,64,1024]{4,3,2,1,0:T(8,128)(2,1)} %all-to-all-done), kind=kLoop, calls=%fused_computation | loop fusion | flops 49283072 | bytes 37748736 | tf_op jit(solution)/shard_map/reduce_sum | solution.py:47
  559.3 8.1 %copy.38 = f32[16,64,1024]{1,0,2:T(8,128)} copy(f32[16,64,1024]{2,1,0:T(8,128)} %multiply_reduce_fusion) | data formatting | bytes 8388608 | tf_op jit(solution)/shard_map/reduce_sum | solution.py:47
  567.3 7.6 reduce_sum.56
  575.0 3.1 reduce_sum.57
  578.1 77.6 %copy.35 = bf16[2,8,16,64,1024]{3,2,4,1,0:T(8,128)(2,1)} copy(bf16[2,8,16,64,1024]{4,3,1,0,2:T(8,128)(2,1)} %bitcast.5) | data formatting | bytes 67108864 | tf_op jit(solution)/shard_map/reshape | solution.py:36
  655.7 86.9 %reshape_reshape.3 = bf16[2,8,1024,64,16]{2,4,3,1,0:T(8,128)(2,1)} reshape(bf16[2,8,16,64,1024]{3,2,4,1,0:T(8,128)(2,1)} %copy.35) | data formatting | bytes 67108864 | tf_op jit(solution)/shard_map/reshape;reshape | solution.py:40
  742.6 25.2 %fusion.5 = f32[64,128,1024]{2,1,0:T(8,128)} fusion(bf16[2,8,1024,64,16]{2,4,3,1,0:T(8,128)(2,1)} %reshape_reshape.3, bf16[1,8,64,64,16]{2,4,0,3,1:T(8,128)(2,1)} %bitcast.31, bf16[1,8,64,64,16]{2,4,0,3,1:T(8,128)(2,1)S(1)} %bitcast.30, bf16[2,8,64,64,16]{2,4,3,1,0:T(8,128)(2,1)} %bitcast.29), kind=kOutput, calls=%fused_computation.8 | convolution fusion | flops 4307550208 | bytes 71303168 | tf_op jit(solution)/shard_map/pkinw,pkjnw->nij/dot_general | solution.py:41
  767.8 11.9 %fusion.4 = f32[64,1024]{1,0:T(8,128)S(1)} fusion(f32[64,128,1024]{2,1,0:T(8,128)} %fusion.5, f32[64,1024]{1,0:T(8,128)S(1)} %add_bitcast_fusion, f32[64,64]{1,0:T(8,128)S(1)} %add_bitcast_fusion.1), kind=kLoop, calls=%fused_computation.7 | loop fusion | flops 25100288 | bytes 34095104 | tf_op jit(solution)/shard_map/reduce_sum | solution.py:51
  779.7 0.1 bitcast_select_fusion
  779.9 0.1 copy.39
  779.9 11.6 %all_to_all.10 = f32[8,64,128]{2,1,0:T(8,128)S(1)} all-to-all(f32[8,64,128]{2,1,0:T(8,128)S(1)} %copy.39), channel_id=1, replica_groups=mesh['band'=8,'chan'=16] {'band'}, dimensions={0} | all-to-all | bytes 524288 | tf_op jit(solution)/shard_map/all_to_all | solution.py:19
  791.5 0.6 broadcast_multiply_fusion
  (6 shorter events, 0.1 us)
Async XLA Ops:
  12.2 8.2 %copy-start = (bf16[2,8,64,1024]{3,2,1,0:T(8,128)(2,1)S(1)}, bf16[2,8,64,1024]{3,2,1,0:T(8,128)(2,1)}, u32[]{:S(2)}) copy-start(bf16[2,8,64,1024]{3,2,1,0:T(8,128)(2,1)} %param.1) | copy-start | bytes 6291460
  12.2 533.5 %all-to-all-start = ((bf16[16,2,8,64,1024]{4,3,2,1,0:T(8,128)(2,1)}), bf16[16,2,8,64,1024]{4,3,2,1,0:T(8,128)(2,1)}, u32[]{:S(2)}, u32[]{:S(2)}) async-start(bf16[16,2,8,64,1024]{4,3,2,1,0:T(8,128)(2,1)} %stack.5), calls=%async_computation | async-start | bytes 67108864 | tf_op jit(solution)/shard_map/all_to_all | solution.py:37
